TPU v7x, 32 devices: a whole 2x2x4 slice. The times are simulated.
32 devices in a mesh: dp: 8 (over z, core), mp: 4 (over y, x).
Axes of the slice: x: 2, y: 2, z: 4, core: 2. Of those that a mesh axis runs over, the one named last changes fastest.
Arguments:
- token_ids: int32 [8192], P('dp'), may hold values from 0 to 128255
- lengths: int32 [64], P('dp'), may hold values from 1 to 128
- embed_grads: bfloat16 [8192, 4096], P('dp', 'mp'), may hold values from -6 to 6
- vocab_basis: bfloat16 [128256, 32], P('mp'), may hold values from -6 to 6
- embed_basis: bfloat16 [4096, 32], P('mp'), may hold values from -0.09375 to 0.09375
- layer_inputs: bfloat16 [1, 8192, 4096], P(None, 'dp', 'mp'), may hold values from -6 to 6
- layer_grads: bfloat16 [1, 8192, 4096], P(None, 'dp', 'mp'), may hold values from -6 to 6
- input_basis: bfloat16 [1, 4096, 32], P(None, 'mp'), may hold values from -0.09375 to 0.09375
- output_basis: bfloat16 [1, 4096, 32], P(None, 'mp'), may hold values from -0.09375 to 0.09375
- queries: bfloat16 [2, 1024, 256], P(None, 'mp', 'dp'), may hold values from -0.19921875 to 0.19921875
Outputs:
- scores: float32 [64, 256], P('dp')
All inputs are finite; a program needn't handle non-finite values.
Results may differ from a plain program's by a relative error of at most 0.0003.
Values may be sent and summed in bfloat16 or wider, within the bound.
No kernel may reach another device: no remote copies, remote signals or barrier semaphores. Data moves between devices by JAX's collectives and lax.ppermute only.
A program may use at most 64 MiB of HBM per device.

v0:
```python
import jax
import jax.numpy as jnp
from jax import lax
from jax.sharding import PartitionSpec as P

ITERS = 2
damping = 0.01
epsilon = 1e-06
highest = lax.Precision.HIGHEST


def solve_columns(right_side, apply_operator, column_norm, column_curve):
    solution = jnp.zeros_like(right_side)
    residual = right_side
    direction = right_side
    norm_now = column_norm(residual)
    for iteration in range(ITERS):
        images = apply_operator(direction)
        step_size = norm_now / (column_curve(direction, images) + epsilon)
        solution = solution + step_size[:, None, :] * direction
        residual = residual - step_size[:, None, :] * images
        norm_next = column_norm(residual)
        direction = residual + (norm_next / (norm_now + epsilon))[:, None, :] * direction
        norm_now = norm_next
    return solution


def per_device(
    token_ids,
    lengths,
    embed_grads,
    vocab_basis,
    embed_basis,
    layer_inputs,
    layer_grads,
    input_basis,
    output_basis,
    queries,
):
    vocab_rows = vocab_basis.shape[0]
    basis_rank = embed_basis.shape[1]
    layer_count = layer_inputs.shape[0] + 1
    seq_count = lengths.shape[0]
    token_count = token_ids.shape[0]
    slot_len = token_count // seq_count
    sketch_len = basis_rank * basis_rank
    mp_index = lax.axis_index("mp")
    local_ids = token_ids - mp_index * vocab_rows
    inside = (local_ids >= 0) & (local_ids < vocab_rows)
    looked = jnp.take(vocab_basis, jnp.clip(local_ids, 0, vocab_rows - 1), axis=0)
    pieces = [
        jnp.dot(embed_grads, embed_basis, preferred_element_type=jnp.float32),
        jnp.where(inside[:, None], looked.astype(jnp.float32), 0.0),
    ]
    pieces.append(jnp.dot(layer_grads[0], output_basis[0], preferred_element_type=jnp.float32))
    pieces.append(jnp.dot(layer_inputs[0], input_basis[0], preferred_element_type=jnp.float32))
    projected = jnp.concatenate(pieces, axis=1)
    inverse_len = 1.0 / lengths.astype(jnp.float32)
    summed = lax.psum(projected, "mp")
    layout = summed.reshape(seq_count, slot_len, layer_count, 2, basis_rank)
    position = jnp.arange(slot_len, dtype=jnp.int32)
    weights = jnp.where(position[None, :] < lengths[:, None], inverse_len[:, None], 0.0)
    weighted = layout[:, :, :, 0, :] * weights[:, :, None, None]
    sketches = jnp.einsum(
        "stli,stlj->lsij", weighted, layout[:, :, :, 1, :], precision=highest
    ).reshape(layer_count, seq_count, sketch_len)
    examples = seq_count * lax.axis_size("dp")
    targets = lax.all_gather(queries, "dp", axis=2, tiled=True)
    everyone = lax.all_gather(sketches, "dp", axis=1, tiled=True)
    columns = lax.all_to_all(targets, "mp", split_axis=2, concat_axis=1, tiled=True)

    def apply_sketch(direction):
        inner_sums = jnp.einsum("lek,lkq->leq", everyone, direction, precision=highest)
        back_proj = jnp.einsum("lek,leq->lkq", everyone, inner_sums, precision=highest)
        return back_proj / examples + damping * direction

    def local_norm(residual):
        return jnp.sum(residual * residual, axis=1)

    def local_curve(direction, images):
        return jnp.sum(direction * images, axis=1)

    solution = solve_columns(columns.astype(jnp.float32), apply_sketch, local_norm, local_curve)
    partial_value = jnp.einsum("lek,lkq->eq", sketches, solution, precision=highest)
    scores = lax.all_gather(partial_value, "mp", axis=1, tiled=True)
    return scores


def solution(mesh):
    placed = (
        P("dp"),
        P("dp"),
        P("dp", "mp"),
        P("mp", None),
        P("mp", None),
        P(None, "dp", "mp"),
        P(None, "dp", "mp"),
        P(None, "mp", None),
        P(None, "mp", None),
        P(None, "mp", "dp"),
    )
    return jax.shard_map(
        per_device, mesh=mesh, in_specs=placed, out_specs=P("dp", None), check_vma=False
    )
```

profile of v0, /device:TPU:0, one launch (start us, length us, event | category | flops | bytes accessed | tf_op | source)
XLA Modules:
  0.0 111.8 jit_solution(4883537781208353662)
XLA Ops:
  6.5 0.8 compare_and_fusion.1
  7.4 0.7 fusion.25
  8.1 7.3 %copy.30 = bf16[32064,32]{1,0:T(8,128)(2,1)} copy(bf16[32064,32]{0,1:T(8,128)(2,1)} %param.13) | data formatting | bytes 4104192 | tf_op args[3]
  15.4 7.3 %gather_fusion = bf16[1024,32]{1,0:T(8,128)(2,1)S(1)} fusion(bf16[32064,32]{1,0:T(8,128)(2,1)} %copy.30, s32[1024]{0:T(1024)S(1)} %fusion.25), kind=kCustom, calls=%fused_computation | custom fusion | bytes 135168 | tf_op jit(solution)/shard_map/jit(_take)/gather | solution.py:50
  22.8 0.7 fusion
  23.6 0.8 copy-done.1
  24.4 0.7 fusion.2
  25.1 0.7 fusion.26
  26.1 0.9 copy.32
  27.0 17.0 %all_gather.9 = bf16[2,256,256]{1,0,2:T(2,128)(2,1)} all-gather(bf16[2,256,32]{1,0,2:T(2,128)(2,1)S(1)} %copy.28), channel_id=1, replica_groups=mesh['dp'=8,'mp'=4] {'dp'}, dimensions={2}, use_global_device_ids=true | all-gather | bytes 294912 | tf_op jit(solution)/shard_map/all_gather | solution.py:68
  44.0 3.7 %all-to-all-start = ((bf16[2,256,256]{1,0,2:T(2,128)(2,1)}), bf16[2,256,256]{1,0,2:T(2,128)(2,1)S(1)}, u32[]{:S(2)}, u32[]{:S(2)}) async-start(bf16[2,256,256]{1,0,2:T(2,128)(2,1)} %all_gather.9), calls=%async_computation | async-start | bytes 524288 | tf_op jit(solution)/shard_map/all_to_all | solution.py:70
  47.8 5.8 %all-to-all-done = bf16[2,256,256]{1,0,2:T(2,128)(2,1)S(1)} async-done(((bf16[2,256,256]{1,0,2:T(2,128)(2,1)}), bf16[2,256,256]{1,0,2:T(2,128)(2,1)S(1)}, u32[]{:S(2)}, u32[]{:S(2)}) %all-to-all-start) | async-done | bytes 262176 | tf_op jit(solution)/shard_map/all_to_all | solution.py:70
  54.0 0.6 multiply_reduce_fusion.1
  54.6 21.5 %all-reduce.2.cloned.1.call-done = f32[8,128,2,2,32]{1,4,0,2,3:T(8,128)} async-done(((f32[8,128,2,2,32]{1,4,0,2,3:T(8,128)}), f32[8,128,2,2,32]{1,4,0,2,3:T(8,128)}) %all-reduce.2.cloned.1.call-update) | async-done | bytes 524304 | tf_op jit(solution)/shard_map/psum | solution.py:59
  76.0 1.6 %fusion.13 = f32[2,8,32,32]{3,2,1,0:T(8,128)S(1)} fusion(f32[8,128,2,2,32]{1,4,0,2,3:T(8,128)} %all-reduce.2.cloned.1.call-done, f32[8,128]{1,0:T(8,128)S(1)} %fusion.24), kind=kOutput, calls=%fused_computation.25 | convolution fusion | flops 25231360 | bytes 593920 | tf_op jit(solution)/shard_map/stli,stlj->lsij/dot_general | solution.py:64
  77.7 14.7 %all_gather.10 = f32[2,64,1024]{2,1,0:T(8,128)S(1)} all-gather(f32[2,8,1024]{2,1,0:T(8,128)S(1)} %reshape.68), channel_id=1, replica_groups=mesh['dp'=8,'mp'=4] {'dp'}, dimensions={1}, use_global_device_ids=true | all-gather | bytes 589824 | tf_op jit(solution)/shard_map/all_gather | solution.py:69
  92.4 0.4 fusion.27
  92.9 0.8 fusion.8
  93.7 0.2 multiply_reduce_fusion
  93.9 0.7 fusion.19
  94.6 0.8 fusion.7
  95.4 0.7 convolution_bitcast_fusion
  96.1 8.1 %all-gather = f32[4,64,8]{1,2,0:T(8,128)S(1)} all-gather(f32[1,64,8]{1,2,0:T(8,128)S(1)} %convolution_bitcast_fusion), channel_id=1, replica_groups=mesh['dp'=8,'mp'=4] {'mp'}, dimensions={0}, use_global_device_ids=true | all-gather | bytes 10240 | tf_op jit(solution)/shard_map/all_gather | solution.py:85
  104.3 0.7 reshape.79
  (31 shorter events, 1.0 us)
Async XLA Ops:
  6.5 16.2 %copy-start = (bf16[1,1024,1024]{2,1,0:T(8,128)(2,1)S(1)}, bf16[1,1024,1024]{2,1,0:T(8,128)(2,1)}, u32[]{:S(2)}) copy-start(bf16[1,1024,1024]{2,1,0:T(8,128)(2,1)} %param.15) | copy-start | bytes 6291460
  6.5 69.5 %all-reduce.2.cloned.1.call-start = ((), (), s32[]{:S(2)}) async-start(), calls=%async_computation.1 | async-start | bytes 1048576 | tf_op jit(solution)/shard_map/psum | solution.py:59
  15.4 7.4 %copy-start.3 = (bf16[1,1024,32]{1,2,0:T(8,128)(2,1)S(1)}, bf16[1,1024,32]{1,2,0:T(8,128)(2,1)}, u32[]{:S(2)}) copy-start(bf16[1,1024,32]{1,2,0:T(8,128)(2,1)} %param.17) | copy-start | bytes 196612
  15.4 8.2 %copy-start.4 = (bf16[1,1024,32]{1,2,0:T(8,128)(2,1)S(1)}, bf16[1,1024,32]{1,2,0:T(8,128)(2,1)}, u32[]{:S(2)}) copy-start(bf16[1,1024,32]{1,2,0:T(8,128)(2,1)} %param.18) | copy-start | bytes 196612
  22.8 1.6 %copy-start.1 = (bf16[1,1024,1024]{2,1,0:T(8,128)(2,1)S(1)}, bf16[1,1024,1024]{2,1,0:T(8,128)(2,1)}, u32[]{:S(2)}) copy-start(bf16[1,1024,1024]{2,1,0:T(8,128)(2,1)} %param.16) | copy-start | bytes 6291460
  22.8 2.3 %copy-start.2 = (bf16[1024,1024]{1,0:T(8,128)(2,1)S(1)}, bf16[1024,1024]{1,0:T(8,128)(2,1)}, u32[]{:S(2)}) copy-start(bf16[1024,1024]{1,0:T(8,128)(2,1)} %param.12) | copy-start | bytes 6291460
  22.8 2.3 %copy-start.5 = (bf16[1024,32]{0,1:T(8,128)(2,1)S(1)}, bf16[1024,32]{0,1:T(8,128)(2,1)}, u32[]{:S(2)}) copy-start(bf16[1024,32]{0,1:T(8,128)(2,1)} %param.14) | copy-start | bytes 196612
  25.9 1.1 %copy-start.6 = (bf16[2,256,32]{1,2,0:T(8,128)(2,1)S(1)}, bf16[2,256,32]{1,2,0:T(8,128)(2,1)}, u32[]{:S(2)}) copy-start(bf16[2,256,32]{1,2,0:T(8,128)(2,1)} %param.19) | copy-start | bytes 98308
  25.9 21.9 %copy-start.7 = (s32[8]{0:T(128)S(1)}, s32[8]{0:T(128)}, u32[]{:S(2)}) copy-start(s32[8]{0:T(128)} %param.11) | copy-start | bytes 100
  44.0 9.6 %all-to-all-start = ((bf16[2,256,256]{1,0,2:T(2,128)(2,1)}), bf16[2,256,256]{1,0,2:T(2,128)(2,1)S(1)}, u32[]{:S(2)}, u32[]{:S(2)}) async-start(bf16[2,256,256]{1,0,2:T(2,128)(2,1)} %all_gather.9), calls=%async_computation | async-start | bytes 524288 | tf_op jit(solution)/shard_map/all_to_all | solution.py:70
Sparse Core Ops, SparseCore 0:
  27.1 48.8 all-reduce.1
where the time goes:
time: 112 us
  blocking collectives  39.8 us (36%)
  waiting for transfers between devices  27.3 us (24%)
  local copies, waits for them, and re-layouts  17.8 us (16%)
  between operations  13.6 us (12%)
  matrix products  7.11 us (6%)
  starting transfers between devices  3.71 us (3%)
  other arithmetic  2.52 us (2%)
    psum x1, waiting for transfers between devices, per_device(): summed = lax.psum(projected, 'mp')  21.5 us
    all_gather x1, blocking collectives, per_device(): targets = lax.all_gather(queries, 'dp', axis=2, tiled=True)  17 us
    all_gather x1, blocking collectives, per_device(): everyone = lax.all_gather(sketches, 'dp', axis=1, tiled=True)  14.7 us
    unnamed x20, local copies, waits for them, and re-layouts  8.96 us
    all_gather x1, blocking collectives, per_device(): scores = lax.all_gather(partial_value, 'mp', axis=1, tiled=True)  8.14 us
    gather x2, local copies, waits for them, and re-layouts, per_device(): jnp.take(vocab_basis, jnp.clip(local_ids, 0, vocab_rows - 1), axis=0)  7.42 us
    all_to_all x1, waiting for transfers between devices, per_device(): lax.all_to_all(targets, 'mp', split_axis=2, concat_axis=1, tiled=True)  5.79 us
    all_to_all x1, starting transfers between devices, per_device(): lax.all_to_all(targets, 'mp', split_axis=2, concat_axis=1, tiled=True)  3.71 us
  transfers between devices with their start and end apart: 2, of which 2 were waited for; matrix products, arithmetic and copies ran while one was open for 1% of the time, Pallas kernels for 0%

commit v1 on v0

--- a/solution.py
+++ b/solution.py
@@ -56,7 +56,9 @@
     pieces.append(jnp.dot(layer_inputs[0], input_basis[0], preferred_element_type=jnp.float32))
     projected = jnp.concatenate(pieces, axis=1)
     inverse_len = 1.0 / lengths.astype(jnp.float32)
-    summed = lax.psum(projected, "mp")
+    summed = projected
+    for hop in (1, 2):
+        summed = summed + lax.ppermute(summed, "mp", [(dev, dev ^ hop) for dev in range(4)])
     layout = summed.reshape(seq_count, slot_len, layer_count, 2, basis_rank)
     position = jnp.arange(slot_len, dtype=jnp.int32)
     weights = jnp.where(position[None, :] < lengths[:, None], inverse_len[:, None], 0.0)

time: 112 us -> 88.5 us (0.79)
  waiting for transfers between devices: 27.3 us -> 13.1 us
  between operations: 13.6 us -> 0.2 us
  starting transfers between devices: 3.71 us -> 8.48 us
  other arithmetic: 2.52 us -> 4.72 us
  blocking collectives: 39.8 us -> 38.5 us
    psum x1 -> x0, waiting for transfers between devices: 21.5 us -> none  [per_device(): summed = lax.psum(projected, 'mp')]
    ppermute x0 -> x2, waiting for transfers between devices: none -> 9.99 us  [per_device(): lax.ppermute(summed, 'mp', [(dev, dev ^ hop) for dev in range(4)])]
    ppermute x0 -> x2, starting transfers between devices: none -> 5.08 us  [per_device(): lax.ppermute(summed, 'mp', [(dev, dev ^ hop) for dev in range(4)])]
    all_to_all x1, waiting for transfers between devices: 5.79 us -> 3.09 us  [per_device(): lax.all_to_all(targets, 'mp', split_axis=2, concat_axis=1, tiled=True)]
    all_gather x1, blocking collectives: 17 us -> 15.5 us  [per_device(): targets = lax.all_gather(queries, 'dp', axis=2, tiled=True)]
  transfers between devices with their start and end apart: 2 -> 3, of which waited for: 2 -> 2; matrix products, arithmetic and copies ran while one was open for 1% -> 2% of each run, Pallas kernels for 0% -> 0%
where the time goes in v1:
time: 88.5 us; the launch traced here: 88.1 us
  blocking collectives  38.5 us (44%)
  local copies, waits for them, and re-layouts  16.9 us (19%)
  waiting for transfers between devices  13.1 us (15%)
  starting transfers between devices  8.48 us (10%)
  matrix products  6.13 us (7%)
  other arithmetic  4.72 us (5%)
    all_gather x1, blocking collectives, per_device(): targets = lax.all_gather(queries, 'dp', axis=2, tiled=True)  15.5 us
    all_gather x1, blocking collectives, per_device(): everyone = lax.all_gather(sketches, 'dp', axis=1, tiled=True)  14.8 us
    ppermute x2, waiting for transfers between devices, per_device(): lax.ppermute(summed, 'mp', [(dev, dev ^ hop) for dev in range(4)])  9.99 us
    unnamed x20, local copies, waits for them, and re-layouts  8.97 us
    all_gather x1, blocking collectives, per_device(): scores = lax.all_gather(partial_value, 'mp', axis=1, tiled=True)  8.14 us
    gather x2, local copies, waits for them, and re-layouts, per_device(): jnp.take(vocab_basis, jnp.clip(local_ids, 0, vocab_rows - 1), axis=0)  7.42 us
    ppermute x2, starting transfers between devices, per_device(): lax.ppermute(summed, 'mp', [(dev, dev ^ hop) for dev in range(4)])  5.08 us
    all_to_all x1, starting transfers between devices, per_device(): lax.all_to_all(targets, 'mp', split_axis=2, concat_axis=1, tiled=True)  3.4 us
  transfers between devices with their start and end apart: 3, of which 2 were waited for; matrix products, arithmetic and copies ran while one was open for 2% of the time, Pallas kernels for 0%

profile of v1, /device:TPU:0, one launch (start us, length us, event | category | flops | bytes accessed | tf_op | source)
XLA Modules:
  0.0 88.1 jit_solution(1406758532717162953)
XLA Ops:
  0.0 0.8 compare_and_fusion.1
  0.8 0.7 fusion.25
  1.5 7.3 %copy.33 = bf16[32064,32]{1,0:T(8,128)(2,1)} copy(bf16[32064,32]{0,1:T(8,128)(2,1)} %param.13) | data formatting | bytes 4104192 | tf_op args[3]
  8.8 7.3 %gather_fusion = bf16[1024,32]{1,0:T(8,128)(2,1)S(1)} fusion(bf16[32064,32]{1,0:T(8,128)(2,1)} %copy.33, s32[1024]{0:T(1024)S(1)} %fusion.25), kind=kCustom, calls=%fused_computation | custom fusion | bytes 135168 | tf_op jit(solution)/shard_map/jit(_take)/gather | solution.py:50
  16.3 0.7 fusion
  17.0 0.8 copy-done.1
  17.9 0.7 fusion.2
  18.6 0.7 fusion.28
  19.4 3.0 %collective-permute-start = (f32[1024,128]{0,1:T(8,128)S(1)}, f32[1024,128]{0,1:T(8,128)}, u32[]{:S(2)}, u32[]{:S(2)}) collective-permute-start(f32[1024,128]{0,1:T(8,128)S(1)} %pad_maximum_fusion), channel_id=1, source_target_pairs={{0,1},{1,0},{2,3},{3,2},{4,5},{5,4},{6,7},{7,6},{8,9},{9,8},{10,11... | collective-permute-start | bytes 1572872 | tf_op jit(solution)/shard_map/ppermute | solution.py:61
  22.5 15.5 %all_gather.9 = bf16[2,256,256]{1,0,2:T(2,128)(2,1)} all-gather(bf16[2,256,32]{1,0,2:T(2,128)(2,1)S(1)} %copy.31), channel_id=1, replica_groups=mesh['dp'=8,'mp'=4] {'dp'}, dimensions={2}, use_global_device_ids=true | all-gather | bytes 294912 | tf_op jit(solution)/shard_map/all_gather | solution.py:70
  38.0 3.4 %all-to-all-start = ((bf16[2,256,256]{1,0,2:T(2,128)(2,1)}), bf16[2,256,256]{1,0,2:T(2,128)(2,1)S(1)}, u32[]{:S(2)}, u32[]{:S(2)}) async-start(bf16[2,256,256]{1,0,2:T(2,128)(2,1)} %all_gather.9), calls=%async_computation | async-start | bytes 524288 | tf_op jit(solution)/shard_map/all_to_all | solution.py:72
  41.4 1.1 %fusion.26 = f32[1024,128]{0,1:T(8,128)S(1)} fusion(f32[1024,128]{0,1:T(8,128)} %collective-permute-done, f32[1024,32]{0,1:T(8,128)S(1)} %fusion, f32[1024,32]{0,1:T(8,128)S(1)} %fusion.2, f32[1024,32]{0,1:T(8,128)S(1)} %convert_select_fusion, f32[1024,32]{0,1:T(8,128)S(1)} %fusion.28), kind=kLoop, calls=%fused_computation.47 | loop fusion | flops 524288 | bytes 1572864 | tf_op jit(solution)/shard_map/add | solution.py:61
  42.5 2.0 %collective-permute-start.1 = (f32[1024,128]{0,1:T(8,128)S(1)}, f32[1024,128]{0,1:T(8,128)}, u32[]{:S(2)}, u32[]{:S(2)}) collective-permute-start(f32[1024,128]{0,1:T(8,128)S(1)} %fusion.26), channel_id=1, source_target_pairs={{0,2},{1,3},{2,0},{3,1},{4,6},{5,7},{6,4},{7,5},{8,10},{9,11},{10,... | collective-permute-start | bytes 1572872 | tf_op jit(solution)/shard_map/ppermute | solution.py:61
  44.7 3.1 %all-to-all-done = bf16[2,256,256]{1,0,2:T(2,128)(2,1)S(1)} async-done(((bf16[2,256,256]{1,0,2:T(2,128)(2,1)}), bf16[2,256,256]{1,0,2:T(2,128)(2,1)S(1)}, u32[]{:S(2)}, u32[]{:S(2)}) %all-to-all-start) | async-done | bytes 262176 | tf_op jit(solution)/shard_map/all_to_all | solution.py:72
  48.7 10.0 %collective-permute-done.1 = f32[1024,128]{0,1:T(8,128)} collective-permute-done((f32[1024,128]{0,1:T(8,128)S(1)}, f32[1024,128]{0,1:T(8,128)}, u32[]{:S(2)}, u32[]{:S(2)}) %collective-permute-start.1) | collective-permute-done | bytes 524320 | tf_op jit(solution)/shard_map/ppermute | solution.py:61
  58.7 1.1 %add_bitcast_fusion = f32[16,8,8,128]{3,1,2,0:T(8,128)S(1)} fusion(f32[1024,128]{0,1:T(8,128)S(1)} %fusion.26, f32[1024,128]{0,1:T(8,128)} %collective-permute-done.1), kind=kLoop, calls=%fused_computation.24 | loop fusion | flops 131072 | bytes 1572864
  59.9 0.6 fusion.13
  60.7 14.8 %all_gather.10 = f32[2,64,1024]{2,1,0:T(8,128)S(1)} all-gather(f32[2,8,1024]{2,1,0:T(8,128)S(1)} %reshape.68), channel_id=1, replica_groups=mesh['dp'=8,'mp'=4] {'dp'}, dimensions={1}, use_global_device_ids=true | all-gather | bytes 589824 | tf_op jit(solution)/shard_map/all_gather | solution.py:71
  75.9 0.8 fusion.8
  77.0 0.7 fusion.19
  77.7 0.8 fusion.7
  78.5 0.7 convolution_bitcast_fusion
  79.2 8.1 %all-gather = f32[4,64,8]{1,2,0:T(8,128)S(1)} all-gather(f32[1,64,8]{1,2,0:T(8,128)S(1)} %convolution_bitcast_fusion), channel_id=1, replica_groups=mesh['dp'=8,'mp'=4] {'mp'}, dimensions={0}, use_global_device_ids=true | all-gather | bytes 10240 | tf_op jit(solution)/shard_map/all_gather | solution.py:87
  87.4 0.7 reshape.79
  (34 shorter events, 2.3 us)
Async XLA Ops:
  0.0 16.2 %copy-start = (bf16[1,1024,1024]{2,1,0:T(8,128)(2,1)S(1)}, bf16[1,1024,1024]{2,1,0:T(8,128)(2,1)}, u32[]{:S(2)}) copy-start(bf16[1,1024,1024]{2,1,0:T(8,128)(2,1)} %param.15) | copy-start | bytes 6291460
  8.8 7.4 %copy-start.3 = (bf16[1,1024,32]{1,2,0:T(8,128)(2,1)S(1)}, bf16[1,1024,32]{1,2,0:T(8,128)(2,1)}, u32[]{:S(2)}) copy-start(bf16[1,1024,32]{1,2,0:T(8,128)(2,1)} %param.17) | copy-start | bytes 196612
  8.8 8.2 %copy-start.4 = (bf16[1,1024,32]{1,2,0:T(8,128)(2,1)S(1)}, bf16[1,1024,32]{1,2,0:T(8,128)(2,1)}, u32[]{:S(2)}) copy-start(bf16[1,1024,32]{1,2,0:T(8,128)(2,1)} %param.18) | copy-start | bytes 196612
  16.3 1.6 %copy-start.1 = (bf16[1,1024,1024]{2,1,0:T(8,128)(2,1)S(1)}, bf16[1,1024,1024]{2,1,0:T(8,128)(2,1)}, u32[]{:S(2)}) copy-start(bf16[1,1024,1024]{2,1,0:T(8,128)(2,1)} %param.16) | copy-start | bytes 6291460
  16.3 2.3 %copy-start.2 = (bf16[1024,1024]{1,0:T(8,128)(2,1)S(1)}, bf16[1024,1024]{1,0:T(8,128)(2,1)}, u32[]{:S(2)}) copy-start(bf16[1024,1024]{1,0:T(8,128)(2,1)} %param.12) | copy-start | bytes 6291460
  16.3 2.3 %copy-start.5 = (bf16[1024,32]{0,1:T(8,128)(2,1)S(1)}, bf16[1024,32]{0,1:T(8,128)(2,1)}, u32[]{:S(2)}) copy-start(bf16[1024,32]{0,1:T(8,128)(2,1)} %param.14) | copy-start | bytes 196612
  18.6 3.9 %copy-start.6 = (bf16[2,256,32]{1,2,0:T(8,128)(2,1)S(1)}, bf16[2,256,32]{1,2,0:T(8,128)(2,1)}, u32[]{:S(2)}) copy-start(bf16[2,256,32]{1,2,0:T(8,128)(2,1)} %param.19) | copy-start | bytes 98308
  19.3 25.3 %copy-start.7 = (s32[8]{0:T(128)S(1)}, s32[8]{0:T(128)}, u32[]{:S(2)}) copy-start(s32[8]{0:T(128)} %param.11) | copy-start | bytes 100
  19.4 22.0 %collective-permute-start = (f32[1024,128]{0,1:T(8,128)S(1)}, f32[1024,128]{0,1:T(8,128)}, u32[]{:S(2)}, u32[]{:S(2)}) collective-permute-start(f32[1024,128]{0,1:T(8,128)S(1)} %pad_maximum_fusion), channel_id=1, source_target_pairs={{0,1},{1,0},{2,3},{3,2},{4,5},{5,4},{6,7},{7,6},{8,9},{9,8},{10,11... | collective-permute-start | bytes 1572872 | tf_op jit(solution)/shard_map/ppermute | solution.py:61
  38.0 9.7 %all-to-all-start = ((bf16[2,256,256]{1,0,2:T(2,128)(2,1)}), bf16[2,256,256]{1,0,2:T(2,128)(2,1)S(1)}, u32[]{:S(2)}, u32[]{:S(2)}) async-start(bf16[2,256,256]{1,0,2:T(2,128)(2,1)} %all_gather.9), calls=%async_computation | async-start | bytes 524288 | tf_op jit(solution)/shard_map/all_to_all | solution.py:72
  42.5 16.1 %collective-permute-start.1 = (f32[1024,128]{0,1:T(8,128)S(1)}, f32[1024,128]{0,1:T(8,128)}, u32[]{:S(2)}, u32[]{:S(2)}) collective-permute-start(f32[1024,128]{0,1:T(8,128)S(1)} %fusion.26), channel_id=1, source_target_pairs={{0,2},{1,3},{2,0},{3,1},{4,6},{5,7},{6,4},{7,5},{8,10},{9,11},{10,... | collective-permute-start | bytes 1572872 | tf_op jit(solution)/shard_map/ppermute | solution.py:61
